TPU v7x, 32 devices: a whole 2x2x4 slice. The times are simulated.
32 devices in a mesh: gx: 4 (over z), gy: 8 (over y, x, core).
Axes of the slice: x: 2, y: 2, z: 4, core: 2. Of those that a mesh axis runs over, the one named last changes fastest.
Arguments:
- rhs: float32 [4, 8, 1, 3, 200, 128], P('gx', 'gy'), may hold values from -25 to 25
- stiff_inverse: bfloat16 [4, 8, 1, 1200, 1200], P('gx', 'gy'), may hold values from -2 to 6, as said below
- schur: bfloat16 [4, 8, 1, 1200, 1200], P('gx', 'gy'), may hold values from -2 to 6, as said below
- phi: bfloat16 [4, 8, 1, 24, 1200], P('gx', 'gy'), may hold values from -0.1875 to 0.1875
- coarse_inverse: float32 [192, 192], P(('gx', 'gy')), may hold values from -2 to 6, as said below
- incidence: int32 [4, 8, 1, 8], P('gx', 'gy'), may hold values from 0 to 63, as said below
- pairing: int32 [4, 8, 1, 3, 200], P('gx', 'gy'), may hold values from 0 to 199, as said below
Outputs:
- multipliers: float32 [4, 8, 1, 3, 200, 128], P('gx', 'gy')
- reduction: float32 [128], replicated
Inputs may be any that keep to these rules, and one draw needn't show every extreme that they name: `stiff_inverse`: each block is symmetric positive definite. `schur`: each block is symmetric positive definite. `coarse_inverse`: symmetric positive definite. `incidence`: the corners of the subdomain grid, periodic in the first two dimensions, under an arbitrary numbering of the 64 nodes: corner c of subdomain (x, y, z) is the grid point (x + c % 2, y + (c // 2) % 2, z + c // 4), and subdomains that share a grid point name the same node. `pairing`: each row over the last dimension is a permutation of 0 to 199.
All inputs are finite; a program needn't handle non-finite values.
Results may differ from a plain program's by a relative error of at most 0.0027.
Values sent between devices are 32-bit elements; how exact they have to be, the bound alone decides.
A program may use at most 64 MiB of HBM per device.

v0:
```python
import jax
import jax.numpy as jnp
from jax import lax
from jax.sharding import PartitionSpec as P

ITERS = 2
largest_index = lax.Precision.HIGHEST


def passed_along(array, axis, by):
    peers = lax.axis_size(axis)
    return lax.ppermute(array, axis, [(i, (i + by) % peers) for i in range(peers)])


def local(rhs, stiff_inverse, schur, phi, coarse_inverse, incidence, pairing):
    blocks = rhs.shape[2]
    face_dofs = rhs.shape[4]
    load_cases = rhs.shape[5]
    interface = 6 * face_dofs
    stiffness = stiff_inverse[0, 0]
    schur_block_stack = schur[0, 0]
    coupling_matrix = phi[0, 0].astype(jnp.float32)
    local_ids = incidence[0, 0]
    level = jnp.arange(blocks)[:, None]
    axis_id = jnp.arange(3)[None, :]
    active = jnp.where((level == blocks - 1) & (axis_id == 2), 0.0, 1.0).astype(jnp.float32)[
        :, :, None, None
    ]
    perm_table = (pairing[0, 0][..., None] == jnp.arange(face_dofs)[None, None, None, :]).astype(
        jnp.float32
    )
    owner_weights = None
    own_ids = jnp.concatenate([local_ids[:, 0], local_ids[-1:, 4]])
    own_dofs = (3 * own_ids[:, None] + jnp.arange(3, dtype=jnp.int32)[None, :]).reshape(-1)
    picked = jnp.take(
        lax.all_gather(coarse_inverse, ("gx", "gy"), axis=0, tiled=True), own_dofs, axis=1
    )
    every_owner = lax.all_gather(own_ids, ("gx", "gy"), axis=0, tiled=True)
    gathered_dofs = (3 * every_owner[:, None] + jnp.arange(3, dtype=jnp.int32)[None, :]).reshape(-1)
    owner_weights = jnp.take(picked, gathered_dofs, axis=0)

    def transpose_jump(values):
        masked = values * active
        moved = jnp.einsum("sakj,sakr->sajr", perm_table, masked, precision=largest_index)
        lower_x = passed_along(moved[:, 0], "gx", 1)
        lower_y = passed_along(moved[:, 1], "gy", 1)
        lower_z = jnp.concatenate([jnp.zeros_like(moved[:1, 2]), moved[:-1, 2]], axis=0)
        return jnp.stack(
            [-lower_x, masked[:, 0], -lower_y, masked[:, 1], -lower_z, masked[:, 2]], axis=1
        )

    def jump_field(field):
        upper_x = passed_along(field[:, 0], "gx", -1)
        upper_y = passed_along(field[:, 2], "gy", -1)
        upper_z = jnp.concatenate([field[1:, 4], jnp.zeros_like(field[:1, 4])], axis=0)
        neighbour = jnp.stack([upper_x, upper_y, upper_z], axis=1)
        paired = jnp.einsum("sakj,sajr->sakr", perm_table, neighbour, precision=largest_index)
        higher = jnp.stack([field[:, 1], field[:, 3], field[:, 5]], axis=1)
        return (higher - paired) * active

    def apply_local(matrices, field):
        low_field = field.reshape(blocks, interface, load_cases).astype(jnp.bfloat16)
        result = jnp.einsum("snm,smr->snr", matrices, low_field, preferred_element_type=jnp.float32)
        return result.reshape(blocks, 6, face_dofs, load_cases)

    def precondition(values):
        field = 0.5 * transpose_jump(values)
        return 0.5 * jump_field(apply_local(schur_block_stack, field))

    def inner_product(left, right):
        return jnp.sum(left * right, axis=(0, 1, 2))

    def energy_total(partial_value):
        return lax.psum(partial_value, ("gx", "gy"))

    residual = rhs[0, 0] * active
    multipliers = jnp.zeros_like(residual)
    preconditioned = precondition(residual)
    partial_energy = inner_product(residual, preconditioned)
    energy = energy_total(partial_energy)
    direction_field = None
    search_corner_values = None
    start_energy = energy
    direction = preconditioned
    for iteration in range(ITERS):
        direction_field = transpose_jump(direction)
        split = jnp.einsum(
            "vzh,vhq->vzq",
            coupling_matrix,
            direction_field.reshape(blocks, interface, load_cases),
            precision=largest_index,
        ).reshape(blocks, 2, 2, 2, 3, load_cases)
        empty = jnp.zeros((1, 2, 2, 3, load_cases), jnp.float32)
        by_node = jnp.concatenate([split[:, 0], empty], axis=0) + jnp.concatenate(
            [empty, split[:, 1]], axis=0
        )
        from_x = passed_along(by_node[:, :, 1], "gx", 1)
        along_x = by_node[:, :, 0] + from_x
        from_y = passed_along(along_x[:, 1], "gy", 1)
        owned = (along_x[:, 0] + from_y).reshape(-1, load_cases)
        gathered = lax.all_gather(owned, ("gx", "gy"), axis=0, tiled=True)
        solved = jnp.dot(owner_weights.T, gathered, precision=largest_index).reshape(
            blocks + 1, 3, load_cases
        )
        from_upper_x = passed_along(solved, "gx", -1)
        pair = jnp.stack([solved, from_upper_x], axis=0)
        from_upper_y = passed_along(pair, "gy", -1)
        quad = jnp.stack([pair, from_upper_y], axis=0)
        neighbour_values = jnp.stack([quad[:, :, :blocks], quad[:, :, 1:]], axis=0)
        neighbour_values = jnp.transpose(neighbour_values, (3, 0, 1, 2, 4, 5)).reshape(
            blocks, -1, load_cases
        )
        search_corner_values = neighbour_values
        spread_operator = jnp.einsum(
            "xgy,xgh->xyh", coupling_matrix, search_corner_values, precision=largest_index
        )
        displacement = apply_local(stiffness, direction_field) + spread_operator.reshape(
            blocks, 6, face_dofs, load_cases
        )
        product_field = jump_field(displacement)
        curvature = lax.psum(inner_product(direction, product_field), ("gx", "gy"))
        alpha = energy / curvature
        multipliers = multipliers + alpha * direction
        residual = residual - alpha * product_field
        preconditioned = precondition(residual)
        partial_energy = inner_product(residual, preconditioned)
        if iteration + 1 < ITERS:
            energy_next = energy_total(partial_energy)
            ratio = energy_next / energy
            direction = preconditioned + ratio * direction
        else:
            energy_next = energy_total(partial_energy)
        energy = energy_next
    return (multipliers[None, None], energy / start_energy)


def solution(mesh):
    return jax.shard_map(
        local,
        mesh=mesh,
        in_specs=(
            P("gx", "gy", None, None, None, None),
            P("gx", "gy", None, None, None),
            P("gx", "gy", None, None, None),
            P("gx", "gy", None, None, None),
            P(("gx", "gy"), None),
            P("gx", "gy", None, None),
            P("gx", "gy", None, None, None),
        ),
        out_specs=(P("gx", "gy", None, None, None, None), P()),
        check_vma=False,
    )
```

profile of v0, /device:TPU:0, one launch (start us, length us, event | category | flops | bytes accessed | tf_op | source)
XLA Modules:
  0.0 463.3 jit_solution(669811901619081959)
XLA Ops:
  4.6 2.6 collective-permute-start
  13.3 40.4 %all-reduce.4 = s32[64]{0:T(128)S(1)} all-reduce(s32[64]{0:T(128)S(1)} %fusion.96), channel_id=1, replica_groups=mesh['gx'=4,'gy'=8] {'gx','gy'}, use_global_device_ids=true, to_apply=%add.4 | all-reduce | flops 64 | bytes 512
  53.9 41.3 %all-gather = f32[32,6,192]{2,1,0:T(8,128)S(1)} all-gather(f32[1,6,192]{2,1,0:T(8,128)} %bitcast.317), channel_id=1, replica_groups=mesh['gx'=4,'gy'=8] {'gx','gy'}, dimensions={0}, use_global_device_ids=true | all-gather | bytes 152064 | tf_op jit(solution)/shard_map/all_gather | solution.py:36
  103.6 2.8 fusion
  106.6 5.0 %collective-permute-done.2 = f32[1,200,128]{2,1,0:T(8,128)S(1)} collective-permute-done((f32[1,200,128]{2,1,0:T(8,128)S(1)}, f32[1,200,128]{2,1,0:T(8,128)S(1)}, u32[]{:S(2)}, u32[]{:S(2)}) %collective-permute-start.2) | collective-permute-done | bytes 102432 | tf_op jit(solution)/shard_map/ppermute | solution.py:12
  114.1 5.6 %collective-permute-done.4 = f32[1,200,128]{2,1,0:T(8,128)S(1)} collective-permute-done((f32[1,200,128]{2,1,0:T(8,128)S(1)}, f32[1,200,128]{2,1,0:T(8,128)S(1)}, u32[]{:S(2)}, u32[]{:S(2)}) %collective-permute-start.4) | collective-permute-done | bytes 102432 | tf_op jit(solution)/shard_map/ppermute | solution.py:12
  121.6 4.9 %collective-permute-done.6 = f32[2,2,3,128]{3,2,1,0:T(4,128)S(1)} collective-permute-done((f32[2,2,3,128]{3,2,1,0:T(4,128)S(1)}, f32[2,2,3,128]{3,2,1,0:T(4,128)S(1)}, u32[]{:S(2)}, u32[]{:S(2)}) %collective-permute-start.6) | collective-permute-done | bytes 6176 | tf_op jit(solution)/shard_map/ppermute | solution.py:12
  132.0 39.4 %all-gather.1 = f32[32,6,128]{2,1,0:T(8,128)} all-gather(f32[1,6,128]{2,1,0:T(8,128)S(1)} %reshape.812), channel_id=1, replica_groups=mesh['gx'=4,'gy'=8] {'gx','gy'}, dimensions={0}, use_global_device_ids=true | all-gather | bytes 101376 | tf_op jit(solution)/shard_map/all_gather | solution.py:101
  173.6 3.6 collective-permute-done.8
  184.4 3.2 collective-permute-start.10
  193.0 38.4 %all-reduce.5 = (f32[128]{0:T(128)S(1)}, f32[128]{0:T(128)S(1)}) all-reduce(f32[128]{0:T(128)S(1)} %get-tuple-element.3, f32[128]{0:T(128)S(1)} %get-tuple-element.2), channel_id=1, replica_groups=mesh['gx'=4,'gy'=8] {'gx','gy'}, use_global_device_ids=true, to_apply=%region_1.2 | all-reduce | flops 256 | bytes 2048 | tf_op jit(solution)/shard_map/psum | solution.py:74
  234.4 2.2 collective-permute-start.12
  236.6 4.3 collective-permute-done.12
  244.5 3.0 collective-permute-done.14
  249.3 39.4 %psum.37 = f32[128]{0:T(128)S(1)} all-reduce(f32[128]{0:T(128)} %get-tuple-element.65), channel_id=1, replica_groups=mesh['gx'=4,'gy'=8] {'gx','gy'}, use_global_device_ids=true, to_apply=%region_5.6 | all-reduce | flops 128 | bytes 1024 | tf_op jit(solution)/shard_map/psum | solution.py:74
  292.7 4.5 collective-permute-done.16
  300.4 4.1 collective-permute-done.18
  304.5 3.9 collective-permute-done.19
  308.4 40.7 %all-gather.2 = f32[32,6,128]{2,1,0:T(8,128)} all-gather(f32[1,6,128]{2,1,0:T(8,128)S(1)} %reshape.814), channel_id=1, replica_groups=mesh['gx'=4,'gy'=8] {'gx','gy'}, dimensions={0}, use_global_device_ids=true | all-gather | bytes 101376 | tf_op jit(solution)/shard_map/all_gather | solution.py:101
  352.0 3.6 collective-permute-done.20
  368.1 38.5 %psum.38 = f32[128]{0:T(128)S(1)} all-reduce(f32[128]{0:T(128)S(1)} %get-tuple-element.67), channel_id=1, replica_groups=mesh['gx'=4,'gy'=8] {'gx','gy'}, use_global_device_ids=true, to_apply=%region_7.8 | all-reduce | flops 128 | bytes 1024 | tf_op jit(solution)/shard_map/psum | solution.py:121
  411.8 4.3 collective-permute-done.24
  419.7 3.0 collective-permute-done.26
  423.2 39.6 %psum.39 = f32[128]{0:T(128)S(1)} all-reduce(f32[128]{0:T(128)S(1)} %fusion.16), channel_id=1, replica_groups=mesh['gx'=4,'gy'=8] {'gx','gy'}, use_global_device_ids=true, to_apply=%region_9.10 | all-reduce | flops 128 | bytes 1024 | tf_op jit(solution)/shard_map/psum | solution.py:74
  (223 shorter events, 83.9 us)
Async XLA Ops:
  4.1 96.7 %collective-permute-start.1 = (f32[1,200,128]{2,1,0:T(8,128)S(1)}, f32[1,200,128]{2,1,0:T(8,128)}, u32[]{:S(2)}, u32[]{:S(2)}) collective-permute-start(f32[1,200,128]{2,1,0:T(8,128)S(1)} %get-tuple-element.47), channel_id=1, source_target_pairs={{0,1},{1,2},{2,3},{3,4},{4,5},{5,6},{6,7},{7,0},{8,9},{9,10},{10,1... | collective-permute-start | bytes 307208 | tf_op jit(solution)/shard_map/ppermute | solution.py:12
  4.6 94.4 %collective-permute-start = (f32[1,200,128]{2,1,0:T(8,128)}, f32[1,200,128]{2,1,0:T(8,128)}, u32[]{:S(2)}, u32[]{:S(2)}) collective-permute-start(f32[1,200,128]{2,1,0:T(8,128)} %get-tuple-element.48), channel_id=1, source_target_pairs={{0,8},{8,16},{16,24},{24,0},{1,9},{9,17},{17,25},{25,1},{2,10},{10... | collective-permute-start | bytes 307208 | tf_op jit(solution)/shard_map/ppermute | solution.py:12
  106.5 5.2 %collective-permute-start.2 = (f32[1,200,128]{2,1,0:T(8,128)S(1)}, f32[1,200,128]{2,1,0:T(8,128)S(1)}, u32[]{:S(2)}, u32[]{:S(2)}) collective-permute-start(f32[1,200,128]{2,1,0:T(8,128)S(1)} %get-tuple-element.34), channel_id=1, source_target_pairs={{0,24},{8,0},{16,8},{24,16},{1,25},{9,1},{17,9},{25,17},{2,26},{10... | collective-permute-start | bytes 307208 | tf_op jit(solution)/shard_map/ppermute | solution.py:12
  106.6 5.1 %collective-permute-start.3 = (f32[1,200,128]{2,1,0:T(8,128)S(1)}, f32[1,200,128]{2,1,0:T(8,128)S(1)}, u32[]{:S(2)}, u32[]{:S(2)}) collective-permute-start(f32[1,200,128]{2,1,0:T(8,128)S(1)} %get-tuple-element.35), channel_id=1, source_target_pairs={{0,7},{1,0},{2,1},{3,2},{4,3},{5,4},{6,5},{7,6},{8,15},{9,8},{10,9... | collective-permute-start | bytes 307208 | tf_op jit(solution)/shard_map/ppermute | solution.py:12
  113.1 6.5 %collective-permute-start.4 = (f32[1,200,128]{2,1,0:T(8,128)S(1)}, f32[1,200,128]{2,1,0:T(8,128)S(1)}, u32[]{:S(2)}, u32[]{:S(2)}) collective-permute-start(f32[1,200,128]{2,1,0:T(8,128)S(1)} %get-tuple-element.46), channel_id=1, source_target_pairs={{0,8},{8,16},{16,24},{24,0},{1,9},{9,17},{17,25},{25,1},{2,10},{10... | collective-permute-start | bytes 307208 | tf_op jit(solution)/shard_map/ppermute | solution.py:12
  113.3 6.4 %collective-permute-start.5 = (f32[1,200,128]{2,1,0:T(8,128)S(1)}, f32[1,200,128]{2,1,0:T(8,128)S(1)}, u32[]{:S(2)}, u32[]{:S(2)}) collective-permute-start(f32[1,200,128]{2,1,0:T(8,128)S(1)} %get-tuple-element.45), channel_id=1, source_target_pairs={{0,1},{1,2},{2,3},{3,4},{4,5},{5,6},{6,7},{7,0},{8,9},{9,10},{10,1... | collective-permute-start | bytes 307208 | tf_op jit(solution)/shard_map/ppermute | solution.py:12
  120.9 5.5 %collective-permute-start.6 = (f32[2,2,3,128]{3,2,1,0:T(4,128)S(1)}, f32[2,2,3,128]{3,2,1,0:T(4,128)S(1)}, u32[]{:S(2)}, u32[]{:S(2)}) collective-permute-start(f32[2,2,3,128]{3,2,1,0:T(4,128)S(1)} %fusion.85), channel_id=1, source_target_pairs={{0,8},{8,16},{16,24},{24,0},{1,9},{9,17},{17,25},{25,1},{2,10},{10... | collective-permute-start | bytes 18440 | tf_op jit(solution)/shard_map/ppermute | solution.py:12
  127.0 4.2 collective-permute-start.7
  173.5 3.7 collective-permute-start.8
  184.4 5.8 %collective-permute-start.10 = (f32[1,200,128]{2,1,0:T(8,128)S(1)}, f32[1,200,128]{2,1,0:T(8,128)S(1)}, u32[]{:S(2)}, u32[]{:S(2)}) collective-permute-start(f32[1,200,128]{2,1,0:T(8,128)S(1)} %get-tuple-element.29), channel_id=1, source_target_pairs={{0,24},{8,0},{16,8},{24,16},{1,25},{9,1},{17,9},{25,17},{2,26},{10... | collective-permute-start | bytes 307208 | tf_op jit(solution)/shard_map/ppermute | solution.py:12
  187.5 4.2 collective-permute-start.11
  234.4 6.5 %collective-permute-start.12 = (f32[1,200,128]{2,1,0:T(8,128)S(1)}, f32[1,200,128]{2,1,0:T(8,128)S(1)}, u32[]{:S(2)}, u32[]{:S(2)}) collective-permute-start(f32[1,200,128]{2,1,0:T(8,128)S(1)} %get-tuple-element.44), channel_id=1, source_target_pairs={{0,8},{8,16},{16,24},{24,0},{1,9},{9,17},{17,25},{25,1},{2,10},{10... | collective-permute-start | bytes 307208 | tf_op jit(solution)/shard_map/ppermute | solution.py:12
  236.6 5.0 %collective-permute-start.13 = (f32[1,200,128]{2,1,0:T(8,128)S(1)}, f32[1,200,128]{2,1,0:T(8,128)S(1)}, u32[]{:S(2)}, u32[]{:S(2)}) collective-permute-start(f32[1,200,128]{2,1,0:T(8,128)S(1)} %get-tuple-element.43), channel_id=1, source_target_pairs={{0,1},{1,2},{2,3},{3,4},{4,5},{5,6},{6,7},{7,0},{8,9},{9,10},{10,1... | collective-permute-start | bytes 307208 | tf_op jit(solution)/shard_map/ppermute | solution.py:12
  242.7 4.7 %collective-permute-start.14 = (f32[1,200,128]{2,1,0:T(8,128)S(1)}, f32[1,200,128]{2,1,0:T(8,128)S(1)}, u32[]{:S(2)}, u32[]{:S(2)}) collective-permute-start(f32[1,200,128]{2,1,0:T(8,128)S(1)} %get-tuple-element.24), channel_id=1, source_target_pairs={{0,24},{8,0},{16,8},{24,16},{1,25},{9,1},{17,9},{25,17},{2,26},{10... | collective-permute-start | bytes 307208 | tf_op jit(solution)/shard_map/ppermute | solution.py:12
  290.7 6.5 %collective-permute-start.16 = (f32[1,200,128]{2,1,0:T(8,128)S(1)}, f32[1,200,128]{2,1,0:T(8,128)S(1)}, u32[]{:S(2)}, u32[]{:S(2)}) collective-permute-start(f32[1,200,128]{2,1,0:T(8,128)S(1)} %get-tuple-element.42), channel_id=1, source_target_pairs={{0,8},{8,16},{16,24},{24,0},{1,9},{9,17},{17,25},{25,1},{2,10},{10... | collective-permute-start | bytes 307208 | tf_op jit(solution)/shard_map/ppermute | solution.py:12
  292.7 5.0 %collective-permute-start.17 = (f32[1,200,128]{2,1,0:T(8,128)S(1)}, f32[1,200,128]{2,1,0:T(8,128)S(1)}, u32[]{:S(2)}, u32[]{:S(2)}) collective-permute-start(f32[1,200,128]{2,1,0:T(8,128)S(1)} %get-tuple-element.41), channel_id=1, source_target_pairs={{0,1},{1,2},{2,3},{3,4},{4,5},{5,6},{6,7},{7,0},{8,9},{9,10},{10,1... | collective-permute-start | bytes 307208 | tf_op jit(solution)/shard_map/ppermute | solution.py:12
  299.0 5.5 %collective-permute-start.18 = (f32[2,2,3,128]{3,2,1,0:T(4,128)S(1)}, f32[2,2,3,128]{3,2,1,0:T(4,128)S(1)}, u32[]{:S(2)}, u32[]{:S(2)}) collective-permute-start(f32[2,2,3,128]{3,2,1,0:T(4,128)S(1)} %fusion.83), channel_id=1, source_target_pairs={{0,8},{8,16},{16,24},{24,0},{1,9},{9,17},{17,25},{25,1},{2,10},{10... | collective-permute-start | bytes 18440 | tf_op jit(solution)/shard_map/ppermute | solution.py:12
  304.5 3.9 collective-permute-start.19
  351.9 3.7 collective-permute-start.20
  360.9 5.3 %collective-permute-start.22 = (f32[1,200,128]{2,1,0:T(8,128)S(1)}, f32[1,200,128]{2,1,0:T(8,128)S(1)}, u32[]{:S(2)}, u32[]{:S(2)}) collective-permute-start(f32[1,200,128]{2,1,0:T(8,128)S(1)} %get-tuple-element.19), channel_id=1, source_target_pairs={{0,24},{8,0},{16,8},{24,16},{1,25},{9,1},{17,9},{25,17},{2,26},{10... | collective-permute-start | bytes 307208 | tf_op jit(solution)/shard_map/ppermute | solution.py:12
  362.8 4.1 collective-permute-start.23
  409.6 6.5 %collective-permute-start.24 = (f32[1,200,128]{2,1,0:T(8,128)S(1)}, f32[1,200,128]{2,1,0:T(8,128)S(1)}, u32[]{:S(2)}, u32[]{:S(2)}) collective-permute-start(f32[1,200,128]{2,1,0:T(8,128)S(1)} %get-tuple-element.40), channel_id=1, source_target_pairs={{0,8},{8,16},{16,24},{24,0},{1,9},{9,17},{17,25},{25,1},{2,10},{10... | collective-permute-start | bytes 307208 | tf_op jit(solution)/shard_map/ppermute | solution.py:12
  411.8 5.0 %collective-permute-start.25 = (f32[1,200,128]{2,1,0:T(8,128)S(1)}, f32[1,200,128]{2,1,0:T(8,128)S(1)}, u32[]{:S(2)}, u32[]{:S(2)}) collective-permute-start(f32[1,200,128]{2,1,0:T(8,128)S(1)} %get-tuple-element.39), channel_id=1, source_target_pairs={{0,1},{1,2},{2,3},{3,4},{4,5},{5,6},{6,7},{7,0},{8,9},{9,10},{10,1... | collective-permute-start | bytes 307208 | tf_op jit(solution)/shard_map/ppermute | solution.py:12
  417.9 4.7 %collective-permute-start.26 = (f32[1,200,128]{2,1,0:T(8,128)S(1)}, f32[1,200,128]{2,1,0:T(8,128)S(1)}, u32[]{:S(2)}, u32[]{:S(2)}) collective-permute-start(f32[1,200,128]{2,1,0:T(8,128)S(1)} %get-tuple-element.14), channel_id=1, source_target_pairs={{0,24},{8,0},{16,8},{24,16},{1,25},{9,1},{17,9},{25,17},{2,26},{10... | collective-permute-start | bytes 307208 | tf_op jit(solution)/shard_map/ppermute | solution.py:12
  (30 other events, 829.7 us)
where the time goes:
time: 465 us; the launch traced here: 463 us
  blocking collectives  318 us (68%)
  waiting for transfers between devices  58.1 us (12%)
  matrix products  24.5 us (5%)
  starting transfers between devices  24.4 us (5%)
  other arithmetic  20.7 us (4%)
  local copies, waits for them, and re-layouts  16.7 us (4%)
    psum x3, blocking collectives, energy_total(): return lax.psum(partial_value, ('gx', 'gy'))  117 us
    all_gather x2, blocking collectives, local(): gathered = lax.all_gather(owned, ('gx', 'gy'), axis=0, tiled=True)  80 us
    ppermute x28, waiting for transfers between devices, passed_along(): lax.ppermute(array, axis, [(i, (i + by) % peers) for i in range(peers)])  58.1 us
    all_gather x1, blocking collectives, local(): lax.all_gather(coarse_inverse, ('gx', 'gy'), axis=0, tiled=True)  41.3 us
    unnamed x1, blocking collectives  40.4 us
    psum x1, blocking collectives, local(): curvature = lax.psum(inner_product(direction, product_field), ('gx', 'gy'))  38.5 us
    ppermute x28, starting transfers between devices, passed_along(): lax.ppermute(array, axis, [(i, (i + by) % peers) for i in range(peers)])  24.4 us
  transfers between devices with their start and end apart: 28, of which 20 were waited for; matrix products, arithmetic and copies ran while one was open for 4% of the time, Pallas kernels for 0%

commit v1 on v0

--- a/solution.py
+++ b/solution.py
@@ -5,6 +5,12 @@
 
 ITERS = 2
 largest_index = lax.Precision.HIGHEST
+
+
+def gather_and_add(x, axis):
+    pieces = lax.all_gather(x, axis, axis=0, tiled=False)
+    acc = pieces.sum(axis=0)
+    return acc
 
 
 def passed_along(array, axis, by):
@@ -71,7 +77,7 @@
         return jnp.sum(left * right, axis=(0, 1, 2))
 
     def energy_total(partial_value):
-        return lax.psum(partial_value, ("gx", "gy"))
+        return gather_and_add(partial_value, ("gx", "gy"))
 
     residual = rhs[0, 0] * active
     multipliers = jnp.zeros_like(residual)

time: 465 us -> 504 us (1.084)
  blocking collectives: 318 us -> 357 us
    all_gather x0 -> x3, blocking collectives: none -> 119 us  [gather_and_add(): pieces = lax.all_gather(x, axis, axis=0, tiled=False)]
    psum x3 -> x0, blocking collectives: 117 us -> none  [energy_total(): return lax.psum(partial_value, ('gx', 'gy'))]
    psum x1 -> x2, blocking collectives: 38.5 us -> 76.8 us  [local(): curvature = lax.psum(inner_product(direction, product_field), ('gx', 'gy'))]
  transfers between devices with their start and end apart: 28 -> 28, of which waited for: 20 -> 18; matrix products, arithmetic and copies ran while one was open for 4% -> 4% of each run, Pallas kernels for 0% -> 0%
where the time goes in v1:
time: 504 us; the launch traced here: 503 us
  blocking collectives  357 us (71%)
  waiting for transfers between devices  62.3 us (12%)
  matrix products  23.9 us (5%)
  other arithmetic  21.5 us (4%)
  starting transfers between devices  20 us (4%)
  local copies, waits for them, and re-layouts  16.6 us (3%)
    all_gather x3, blocking collectives, gather_and_add(): pieces = lax.all_gather(x, axis, axis=0, tiled=False)  119 us
    all_gather x2, blocking collectives, local(): gathered = lax.all_gather(owned, ('gx', 'gy'), axis=0, tiled=True)  80 us
    psum x2, blocking collectives, local(): curvature = lax.psum(inner_product(direction, product_field), ('gx', 'gy'))  76.8 us
    ppermute x28, waiting for transfers between devices, passed_along(): lax.ppermute(array, axis, [(i, (i + by) % peers) for i in range(peers)])  62.3 us
    all_gather x1, blocking collectives, local(): lax.all_gather(coarse_inverse, ('gx', 'gy'), axis=0, tiled=True)  41.3 us
    unnamed x1, blocking collectives  40.4 us
    ppermute x28, starting transfers between devices, passed_along(): lax.ppermute(array, axis, [(i, (i + by) % peers) for i in range(peers)])  20 us
  transfers between devices with their start and end apart: 28, of which 18 were waited for; matrix products, arithmetic and copies ran while one was open for 4% of the time, Pallas kernels for 0%

profile of v1, /device:TPU:0, one launch (start us, length us, event | category | flops | bytes accessed | tf_op | source)
XLA Modules:
  0.0 503.2 jit_solution(6409442317466892802)
XLA Ops:
  4.6 2.6 collective-permute-start
  13.1 40.4 %all-reduce.4 = s32[64]{0:T(128)S(1)} all-reduce(s32[64]{0:T(128)S(1)} %fusion.96), channel_id=1, replica_groups=mesh['gx'=4,'gy'=8] {'gx','gy'}, use_global_device_ids=true, to_apply=%add.4 | all-reduce | flops 64 | bytes 512
  53.8 41.3 %all-gather.4 = f32[32,6,192]{2,1,0:T(8,128)S(1)} all-gather(f32[1,6,192]{2,1,0:T(8,128)} %bitcast.320), channel_id=1, replica_groups=mesh['gx'=4,'gy'=8] {'gx','gy'}, dimensions={0}, use_global_device_ids=true | all-gather | bytes 152064 | tf_op jit(solution)/shard_map/all_gather | solution.py:42
  103.4 2.8 fusion
  106.5 5.0 %collective-permute-done.2 = f32[1,200,128]{2,1,0:T(8,128)S(1)} collective-permute-done((f32[1,200,128]{2,1,0:T(8,128)S(1)}, f32[1,200,128]{2,1,0:T(8,128)S(1)}, u32[]{:S(2)}, u32[]{:S(2)}) %collective-permute-start.2) | collective-permute-done | bytes 102432 | tf_op jit(solution)/shard_map/ppermute | solution.py:18
  113.9 5.6 %collective-permute-done.4 = f32[1,200,128]{2,1,0:T(8,128)S(1)} collective-permute-done((f32[1,200,128]{2,1,0:T(8,128)S(1)}, f32[1,200,128]{2,1,0:T(8,128)S(1)}, u32[]{:S(2)}, u32[]{:S(2)}) %collective-permute-start.4) | collective-permute-done | bytes 102432 | tf_op jit(solution)/shard_map/ppermute | solution.py:18
  121.4 4.8 collective-permute-done.6
  131.8 39.4 %all-gather.5 = f32[32,6,128]{2,1,0:T(8,128)} all-gather(f32[1,6,128]{2,1,0:T(8,128)S(1)} %reshape.821), channel_id=1, replica_groups=mesh['gx'=4,'gy'=8] {'gx','gy'}, dimensions={0}, use_global_device_ids=true | all-gather | bytes 101376 | tf_op jit(solution)/shard_map/all_gather | solution.py:107
  173.4 3.6 collective-permute-done.8
  184.2 3.2 collective-permute-start.10
  192.8 38.4 %psum.14 = f32[128]{0:T(128)S(1)} all-reduce(f32[128]{0:T(128)S(1)} %get-tuple-element.2), channel_id=1, replica_groups=mesh['gx'=4,'gy'=8] {'gx','gy'}, use_global_device_ids=true, to_apply=%region_3.4 | all-reduce | flops 128 | bytes 1024 | tf_op jit(solution)/shard_map/psum | solution.py:127
  231.2 39.9 %all-gather.3 = f32[32,1,128]{2,1,0:T(1,128)S(1)} all-gather(f32[1,1,128]{2,1,0:T(1,128)S(1)} %bitcast.326), channel_id=2, replica_groups=mesh['gx'=4,'gy'=8] {'gx','gy'}, dimensions={0}, use_global_device_ids=true | all-gather | bytes 16896 | tf_op jit(solution)/shard_map/all_gather | solution.py:11
  274.8 6.3 %collective-permute-done.12 = f32[1,200,128]{2,1,0:T(8,128)S(1)} collective-permute-done((f32[1,200,128]{2,1,0:T(8,128)S(1)}, f32[1,200,128]{2,1,0:T(8,128)S(1)}, u32[]{:S(2)}, u32[]{:S(2)}) %collective-permute-start.12) | collective-permute-done | bytes 102432 | tf_op jit(solution)/shard_map/ppermute | solution.py:18
  284.2 2.8 collective-permute-done.14
  288.3 37.8 %all-gather.6 = f32[32,1,128]{2,1,0:T(1,128)} all-gather(f32[1,1,128]{2,1,0:T(1,128)S(1)} %bitcast.328), channel_id=3, replica_groups=mesh['gx'=4,'gy'=8] {'gx','gy'}, dimensions={0}, use_global_device_ids=true | all-gather | bytes 16896 | tf_op jit(solution)/shard_map/all_gather | solution.py:11
  329.3 6.5 %collective-permute-done.16 = f32[1,200,128]{2,1,0:T(8,128)S(1)} collective-permute-done((f32[1,200,128]{2,1,0:T(8,128)S(1)}, f32[1,200,128]{2,1,0:T(8,128)S(1)}, u32[]{:S(2)}, u32[]{:S(2)}) %collective-permute-start.16) | collective-permute-done | bytes 102432 | tf_op jit(solution)/shard_map/ppermute | solution.py:18
  337.2 5.4 %collective-permute-done.18 = f32[2,2,3,128]{3,2,1,0:T(4,128)S(1)} collective-permute-done((f32[2,2,3,128]{3,2,1,0:T(4,128)S(1)}, f32[2,2,3,128]{3,2,1,0:T(4,128)S(1)}, u32[]{:S(2)}, u32[]{:S(2)}) %collective-permute-start.18) | collective-permute-done | bytes 6176 | tf_op jit(solution)/shard_map/ppermute | solution.py:18
  342.7 3.9 collective-permute-done.19
  346.6 40.7 %all-gather.7 = f32[32,6,128]{2,1,0:T(8,128)} all-gather(f32[1,6,128]{2,1,0:T(8,128)S(1)} %reshape.825), channel_id=1, replica_groups=mesh['gx'=4,'gy'=8] {'gx','gy'}, dimensions={0}, use_global_device_ids=true | all-gather | bytes 101376 | tf_op jit(solution)/shard_map/all_gather | solution.py:107
  390.2 3.6 collective-permute-done.20
  406.3 38.4 %psum.15 = f32[128]{0:T(128)S(1)} all-reduce(f32[128]{0:T(128)S(1)} %get-tuple-element.65), channel_id=1, replica_groups=mesh['gx'=4,'gy'=8] {'gx','gy'}, use_global_device_ids=true, to_apply=%region_7.8 | all-reduce | flops 128 | bytes 1024 | tf_op jit(solution)/shard_map/psum | solution.py:127
  450.0 4.3 collective-permute-done.24
  457.9 3.0 collective-permute-done.26
  461.4 41.2 %all-gather.8 = f32[32,1,128]{2,1,0:T(1,128)S(1)} all-gather(f32[1,1,128]{2,1,0:T(1,128)S(1)} %bitcast.327), channel_id=4, replica_groups=mesh['gx'=4,'gy'=8] {'gx','gy'}, dimensions={0}, use_global_device_ids=true | all-gather | bytes 16896 | tf_op jit(solution)/shard_map/all_gather | solution.py:11
  (227 shorter events, 80.8 us)
Async XLA Ops:
  4.1 96.6 %collective-permute-start.1 = (f32[1,200,128]{2,1,0:T(8,128)S(1)}, f32[1,200,128]{2,1,0:T(8,128)}, u32[]{:S(2)}, u32[]{:S(2)}) collective-permute-start(f32[1,200,128]{2,1,0:T(8,128)S(1)} %get-tuple-element.45), channel_id=1, source_target_pairs={{0,1},{1,2},{2,3},{3,4},{4,5},{5,6},{6,7},{7,0},{8,9},{9,10},{10,1... | collective-permute-start | bytes 307208 | tf_op jit(solution)/shard_map/ppermute | solution.py:18
  4.6 94.3 %collective-permute-start = (f32[1,200,128]{2,1,0:T(8,128)}, f32[1,200,128]{2,1,0:T(8,128)}, u32[]{:S(2)}, u32[]{:S(2)}) collective-permute-start(f32[1,200,128]{2,1,0:T(8,128)} %get-tuple-element.46), channel_id=1, source_target_pairs={{0,8},{8,16},{16,24},{24,0},{1,9},{9,17},{17,25},{25,1},{2,10},{10... | collective-permute-start | bytes 307208 | tf_op jit(solution)/shard_map/ppermute | solution.py:18
  106.3 5.2 %collective-permute-start.2 = (f32[1,200,128]{2,1,0:T(8,128)S(1)}, f32[1,200,128]{2,1,0:T(8,128)S(1)}, u32[]{:S(2)}, u32[]{:S(2)}) collective-permute-start(f32[1,200,128]{2,1,0:T(8,128)S(1)} %get-tuple-element.32), channel_id=1, source_target_pairs={{0,24},{8,0},{16,8},{24,16},{1,25},{9,1},{17,9},{25,17},{2,26},{10... | collective-permute-start | bytes 307208 | tf_op jit(solution)/shard_map/ppermute | solution.py:18
  106.4 5.1 %collective-permute-start.3 = (f32[1,200,128]{2,1,0:T(8,128)S(1)}, f32[1,200,128]{2,1,0:T(8,128)S(1)}, u32[]{:S(2)}, u32[]{:S(2)}) collective-permute-start(f32[1,200,128]{2,1,0:T(8,128)S(1)} %get-tuple-element.33), channel_id=1, source_target_pairs={{0,7},{1,0},{2,1},{3,2},{4,3},{5,4},{6,5},{7,6},{8,15},{9,8},{10,9... | collective-permute-start | bytes 307208 | tf_op jit(solution)/shard_map/ppermute | solution.py:18
  112.9 6.5 %collective-permute-start.4 = (f32[1,200,128]{2,1,0:T(8,128)S(1)}, f32[1,200,128]{2,1,0:T(8,128)S(1)}, u32[]{:S(2)}, u32[]{:S(2)}) collective-permute-start(f32[1,200,128]{2,1,0:T(8,128)S(1)} %get-tuple-element.44), channel_id=1, source_target_pairs={{0,8},{8,16},{16,24},{24,0},{1,9},{9,17},{17,25},{25,1},{2,10},{10... | collective-permute-start | bytes 307208 | tf_op jit(solution)/shard_map/ppermute | solution.py:18
  113.1 6.4 %collective-permute-start.5 = (f32[1,200,128]{2,1,0:T(8,128)S(1)}, f32[1,200,128]{2,1,0:T(8,128)S(1)}, u32[]{:S(2)}, u32[]{:S(2)}) collective-permute-start(f32[1,200,128]{2,1,0:T(8,128)S(1)} %get-tuple-element.43), channel_id=1, source_target_pairs={{0,1},{1,2},{2,3},{3,4},{4,5},{5,6},{6,7},{7,0},{8,9},{9,10},{10,1... | collective-permute-start | bytes 307208 | tf_op jit(solution)/shard_map/ppermute | solution.py:18
  120.8 5.5 %collective-permute-start.6 = (f32[2,2,3,128]{3,2,1,0:T(4,128)S(1)}, f32[2,2,3,128]{3,2,1,0:T(4,128)S(1)}, u32[]{:S(2)}, u32[]{:S(2)}) collective-permute-start(f32[2,2,3,128]{3,2,1,0:T(4,128)S(1)} %fusion.85), channel_id=1, source_target_pairs={{0,8},{8,16},{16,24},{24,0},{1,9},{9,17},{17,25},{25,1},{2,10},{10... | collective-permute-start | bytes 18440 | tf_op jit(solution)/shard_map/ppermute | solution.py:18
  126.9 4.2 collective-permute-start.7
  173.3 3.7 collective-permute-start.8
  184.2 5.8 %collective-permute-start.10 = (f32[1,200,128]{2,1,0:T(8,128)S(1)}, f32[1,200,128]{2,1,0:T(8,128)S(1)}, u32[]{:S(2)}, u32[]{:S(2)}) collective-permute-start(f32[1,200,128]{2,1,0:T(8,128)S(1)} %get-tuple-element.27), channel_id=1, source_target_pairs={{0,24},{8,0},{16,8},{24,16},{1,25},{9,1},{17,9},{25,17},{2,26},{10... | collective-permute-start | bytes 307208 | tf_op jit(solution)/shard_map/ppermute | solution.py:18
  187.4 4.2 collective-permute-start.11
  274.1 7.0 %collective-permute-start.12 = (f32[1,200,128]{2,1,0:T(8,128)S(1)}, f32[1,200,128]{2,1,0:T(8,128)S(1)}, u32[]{:S(2)}, u32[]{:S(2)}) collective-permute-start(f32[1,200,128]{2,1,0:T(8,128)S(1)} %get-tuple-element.42), channel_id=1, source_target_pairs={{0,8},{8,16},{16,24},{24,0},{1,9},{9,17},{17,25},{25,1},{2,10},{10... | collective-permute-start | bytes 307208 | tf_op jit(solution)/shard_map/ppermute | solution.py:18
  274.2 6.9 %collective-permute-start.13 = (f32[1,200,128]{2,1,0:T(8,128)S(1)}, f32[1,200,128]{2,1,0:T(8,128)S(1)}, u32[]{:S(2)}, u32[]{:S(2)}) collective-permute-start(f32[1,200,128]{2,1,0:T(8,128)S(1)} %get-tuple-element.41), channel_id=1, source_target_pairs={{0,1},{1,2},{2,3},{3,4},{4,5},{5,6},{6,7},{7,0},{8,9},{9,10},{10,1... | collective-permute-start | bytes 307208 | tf_op jit(solution)/shard_map/ppermute | solution.py:18
  282.3 4.7 collective-permute-start.14
  328.9 7.0 %collective-permute-start.16 = (f32[1,200,128]{2,1,0:T(8,128)S(1)}, f32[1,200,128]{2,1,0:T(8,128)S(1)}, u32[]{:S(2)}, u32[]{:S(2)}) collective-permute-start(f32[1,200,128]{2,1,0:T(8,128)S(1)} %get-tuple-element.40), channel_id=1, source_target_pairs={{0,8},{8,16},{16,24},{24,0},{1,9},{9,17},{17,25},{25,1},{2,10},{10... | collective-permute-start | bytes 307208 | tf_op jit(solution)/shard_map/ppermute | solution.py:18
  329.0 6.9 %collective-permute-start.17 = (f32[1,200,128]{2,1,0:T(8,128)S(1)}, f32[1,200,128]{2,1,0:T(8,128)S(1)}, u32[]{:S(2)}, u32[]{:S(2)}) collective-permute-start(f32[1,200,128]{2,1,0:T(8,128)S(1)} %get-tuple-element.39), channel_id=1, source_target_pairs={{0,1},{1,2},{2,3},{3,4},{4,5},{5,6},{6,7},{7,0},{8,9},{9,10},{10,1... | collective-permute-start | bytes 307208 | tf_op jit(solution)/shard_map/ppermute | solution.py:18
  337.2 5.5 %collective-permute-start.18 = (f32[2,2,3,128]{3,2,1,0:T(4,128)S(1)}, f32[2,2,3,128]{3,2,1,0:T(4,128)S(1)}, u32[]{:S(2)}, u32[]{:S(2)}) collective-permute-start(f32[2,2,3,128]{3,2,1,0:T(4,128)S(1)} %fusion.83), channel_id=1, source_target_pairs={{0,8},{8,16},{16,24},{24,0},{1,9},{9,17},{17,25},{25,1},{2,10},{10... | collective-permute-start | bytes 18440 | tf_op jit(solution)/shard_map/ppermute | solution.py:18
  342.7 3.9 collective-permute-start.19
  390.1 3.7 collective-permute-start.20
  399.1 5.3 %collective-permute-start.22 = (f32[1,200,128]{2,1,0:T(8,128)S(1)}, f32[1,200,128]{2,1,0:T(8,128)S(1)}, u32[]{:S(2)}, u32[]{:S(2)}) collective-permute-start(f32[1,200,128]{2,1,0:T(8,128)S(1)} %get-tuple-element.17), channel_id=1, source_target_pairs={{0,24},{8,0},{16,8},{24,16},{1,25},{9,1},{17,9},{25,17},{2,26},{10... | collective-permute-start | bytes 307208 | tf_op jit(solution)/shard_map/ppermute | solution.py:18
  401.0 4.1 collective-permute-start.23
  447.8 6.5 %collective-permute-start.24 = (f32[1,200,128]{2,1,0:T(8,128)S(1)}, f32[1,200,128]{2,1,0:T(8,128)S(1)}, u32[]{:S(2)}, u32[]{:S(2)}) collective-permute-start(f32[1,200,128]{2,1,0:T(8,128)S(1)} %get-tuple-element.38), channel_id=1, source_target_pairs={{0,8},{8,16},{16,24},{24,0},{1,9},{9,17},{17,25},{25,1},{2,10},{10... | collective-permute-start | bytes 307208 | tf_op jit(solution)/shard_map/ppermute | solution.py:18
  450.0 5.0 collective-permute-start.25
  456.1 4.7 collective-permute-start.26
  (30 other events, 867.6 us)
